TPU v7x, 32 devices: a whole 2x2x4 slice. The times are simulated.
32 devices in a mesh: groups: 2 (over y), expert: 4 (over z), hidden: 4 (over x, core).
Axes of the slice: x: 2, y: 2, z: 4, core: 2. Of those that a mesh axis runs over, the one named last changes fastest.
Arguments:
- tokens: bfloat16 [512, 4096], P(('groups', 'expert'), 'hidden'), parts along dimension 0, may hold values from -6 to 6
- norm_gain: bfloat16 [4096], P('hidden'), may hold values from 0.25 to 1.75
- gate_proj: bfloat16 [64, 768, 4096], P('expert', 'hidden'), may hold values from -0.09375 to 0.09375
- up_proj: bfloat16 [64, 768, 4096], P('expert', 'hidden'), may hold values from -0.09375 to 0.09375
- down_proj: bfloat16 [64, 768, 4096], P('expert', 'hidden'), may hold values from -0.21875 to 0.21875
- expert_ids: int32 [512, 8], P(('groups', 'expert')), parts along dimension 0, may hold values from 0 to 63, as said below
- slot_ids: int32 [512, 8], P(('groups', 'expert')), parts along dimension 0, may hold values from 0 to 11, as said below
- gate_num: int32 [512, 8], P(('groups', 'expert')), parts along dimension 0, may hold values from 1 to 255
Outputs:
- layer_out: bfloat16 [512, 4096], P(('groups', 'expert'), 'hidden'), parts along dimension 0
There are 2 independent parts, one for each index of `groups`. A program takes and returns all parts, laid end to end along the dimension named above; an argument that names none is the same for every part. Nothing has to cross between parts.
Inputs may be any that keep to these rules, and one draw needn't show every extreme that they name: `expert_ids`: each token names 8 different experts. In every aligned block of 64 tokens (the tokens of one index of the expert axis), a quarter of the experts are named by exactly 12 tokens, a quarter by 8 and the other half by 6; some expert is named by 12 tokens in every block. `slot_ids`: within an aligned block of 64 tokens, the routes that name one expert carry the slots 0 up to their count minus 1, each once.
All inputs are finite; a program needn't handle non-finite values.
Results may differ from a plain program's by a relative error of at most 0.0085.
Values may be sent and summed in bfloat16 or wider, within the bound.
A program may use at most 128 MiB of HBM per device.

v0:
```python
import jax
import jax.numpy as jnp
from jax import lax
from jax.sharding import PartitionSpec as P

D = 4096
SPECIALIST_COUNT = 64
CAP = 12
gate_scale = 1.0 / 1024.0


def route_tables(expert_ids, slot_ids, gate_num):
    slot_index = expert_ids * CAP + slot_ids
    columns = lax.broadcasted_iota(jnp.int32, (1, 1, SPECIALIST_COUNT * CAP), 2)
    matches = slot_index[:, :, None] == columns
    placing = jnp.any(matches, axis=1).astype(jnp.bfloat16)
    scaled = gate_num.astype(jnp.float32) * gate_scale
    weights = jnp.sum(jnp.where(matches, scaled[:, :, None], 0.0), axis=1).astype(jnp.bfloat16)
    return (placing, weights)


def normalize(features, gain, total_squares):
    scale = lax.rsqrt(total_squares / D + 0.5)
    return (
        features.astype(jnp.float32) * scale[:, None] * gain.astype(jnp.float32)[None, :]
    ).astype(jnp.bfloat16)


def place_rows(placing, normed, sources):
    outgoing = lax.dot_general(
        placing, normed, (((0,), (0,)), ((), ())), preferred_element_type=jnp.float32
    )
    return outgoing.astype(jnp.bfloat16).reshape(sources, -1, CAP, normed.shape[1])


def on_device(tokens, norm_gain, gate_proj, up_proj, down_proj, expert_ids, slot_ids, gate_num):
    sources = lax.axis_size("expert")
    placing, weights = route_tables(expert_ids, slot_ids, gate_num)
    local_squares = jnp.sum(jnp.square(tokens.astype(jnp.float32)), axis=1)
    squares = lax.psum(local_squares, "hidden")
    normed = normalize(tokens, norm_gain, squares)
    outgoing = place_rows(placing, normed, sources)
    received = lax.all_to_all(outgoing, "expert", split_axis=0, concat_axis=2, tiled=True)[0]
    block_cols = lax.all_gather(received, "hidden", axis=2, tiled=True)
    gate_more = jnp.einsum(
        "ehd,erd->ehr", gate_proj, block_cols, preferred_element_type=jnp.float32
    )
    up_more = jnp.einsum("ehd,erd->ehr", up_proj, block_cols, preferred_element_type=jnp.float32)
    activated = (jax.nn.silu(gate_more) * up_more).astype(jnp.bfloat16)
    partial_value = jnp.einsum(
        "ehr,ehd->erd", activated, down_proj, preferred_element_type=jnp.float32
    ).astype(jnp.bfloat16)
    returned = lax.all_to_all(
        partial_value[None], "expert", split_axis=2, concat_axis=0, tiled=True
    )
    returned = returned.reshape(-1, returned.shape[-1])
    partial_out = jnp.dot(weights, returned, preferred_element_type=jnp.float32)
    return lax.psum_scatter(partial_out, "hidden", scatter_dimension=1, tiled=True).astype(
        jnp.bfloat16
    )


def solution(mesh):
    placed = (
        P(("groups", "expert"), "hidden"),
        P("hidden"),
        P("expert", "hidden", None),
        P("expert", "hidden", None),
        P("expert", "hidden", None),
        P(("groups", "expert"), None),
        P(("groups", "expert"), None),
        P(("groups", "expert"), None),
    )
    return jax.shard_map(
        on_device,
        mesh=mesh,
        in_specs=placed,
        out_specs=P(("groups", "expert"), "hidden"),
        check_vma=False,
    )
```

profile of v0, /device:TPU:0, one launch (start us, length us, event | category | flops | bytes accessed | tf_op | source)
XLA Modules:
  0.0 358.5 jit_solution(16859934131630568120)
XLA Ops:
  6.5 0.0 all-gather.2.cloned.1.call-start
  6.5 0.7 multiply_add_fusion
  7.2 0.1 copy.24
  7.3 0.5 fusion.1
  7.9 0.7 convert_element_type.32
  8.6 1.0 fusion.10
  9.6 8.4 %psum.7 = f32[64]{0:T(128)S(1)} all-reduce(f32[64]{0:T(128)S(1)} %fusion.10), channel_id=1, replica_groups=mesh['groups'=2,'expert'=4,'hidden'=4] {'hidden'}, use_global_device_ids=true, to_apply=%region_3.4 | all-reduce | flops 64 | bytes 512 | tf_op jit(solution)/shard_map/psum | solution.py:40
  18.0 2.7 convolution_convert_fusion.1
  20.7 2.4 reshape.12
  23.1 0.9 copy.26
  23.9 40.4 %all_to_all.30 = bf16[4,16,12,1024]{3,1,2,0:T(8,128)(2,1)S(1)} all-to-all(bf16[4,16,12,1024]{3,1,2,0:T(8,128)(2,1)S(1)} %copy.26), channel_id=1, replica_groups=mesh['groups'=2,'expert'=4,'hidden'=4] {'expert'}, dimensions={0} | all-to-all | bytes 3145728 | tf_op jit(solution)/shard_map/all_to_all | solution.py:43
  64.4 2.0 copy.27
  66.4 0.0 all-gather.2.cloned.1.call-update
  66.4 45.7 %all-gather.2.cloned.1.call-done = bf16[16,48,4096]{2,1,0:T(8,128)(2,1)} async-done(((bf16[16,48,1024]{2,1,0:T(8,128)(2,1)}), bf16[16,48,4096]{2,1,0:T(8,128)(2,1)}) %all-gather.2.cloned.1.call-update) | async-done | bytes 6291472 | tf_op jit(solution)/shard_map/all_gather | solution.py:44
  112.0 14.1 %convolution_bitcast_fusion.1 = f32[16,192,48]{1,2,0:T(8,128)S(1)} fusion(bf16[16,48,4096]{2,1,0:T(8,128)(2,1)} %all-gather.2.cloned.1.call-done, bf16[16,192,4096]{2,1,0:T(8,128)(2,1)} %param.10), kind=kOutput, calls=%fused_computation.7 | convolution fusion | flops 1207959552 | bytes 32047104 | tf_op jit(solution)/shard_map/ehd,erd->ehr/dot_general | solution.py:45
  126.2 22.9 %fusion = bf16[1,16,48,4096]{3,2,1,0:T(8,128)(2,1)} fusion(bf16[16,192,4096]{2,1,0:T(8,128)(2,1)} %param.12, bf16[16,48,4096]{2,1,0:T(8,128)(2,1)} %all-gather.2.cloned.1.call-done, bf16[16,192,4096]{2,1,0:T(8,128)(2,1)} %param.11, f32[16,192,48]{1,2,0:T(8,128)S(1)} %convolution_bitcast_fusion.1), kind=kOutput, calls=%fused_computation.1 | convolution fusion | flops 2419949568 | bytes 63504384 | tf_op jit(solution)/shard_map/ehr,ehd->erd/dot_general | solution.py:50
  149.1 8.9 %copy.28 = bf16[1,16,48,4096]{3,1,0,2:T(8,128)(2,1)} copy(bf16[1,16,48,4096]{3,2,1,0:T(8,128)(2,1)} %fusion) | data formatting | bytes 12582912 | tf_op jit(solution)/shard_map/broadcast_in_dim | solution.py:54
  158.0 0.0 copy-start
  158.0 5.4 %all-to-all-start.1 = ((bf16[1,16,48,4096]{3,1,0,2:T(8,128)(2,1)}), bf16[1,16,48,4096]{3,1,0,2:T(8,128)(2,1)}, u32[]{:S(2)}, u32[]{:S(2)}) async-start(bf16[1,16,48,4096]{3,1,0,2:T(8,128)(2,1)} %copy.28), calls=%async_computation.1 | async-start | bytes 12582912 | tf_op jit(solution)/shard_map/all_to_all | solution.py:53
  163.5 0.3 reduce-scatter.2.cloned.1.call-start
  163.7 0.0 copy-done
  163.7 0.1 copy.25
  163.8 0.6 select_reduce_fusion
  164.4 137.9 %all-to-all-done.1 = bf16[1,16,48,4096]{3,1,0,2:T(8,128)(2,1)} async-done(((bf16[1,16,48,4096]{3,1,0,2:T(8,128)(2,1)}), bf16[1,16,48,4096]{3,1,0,2:T(8,128)(2,1)}, u32[]{:S(2)}, u32[]{:S(2)}) %all-to-all-start.1) | async-done | bytes 6291488 | tf_op jit(solution)/shard_map/all_to_all | solution.py:53
  302.3 9.8 %copy.29 = bf16[4,1,16,12,4096]{4,3,2,0,1:T(8,128)(2,1)} copy(bf16[4,1,16,12,4096]{4,2,3,0,1:T(8,128)(2,1)} %bitcast.7) | data formatting | bytes 12582912 | tf_op jit(solution)/shard_map/all_to_all | solution.py:53
  312.1 9.9 %reshape.13 = bf16[768,4096]{1,0:T(8,128)(2,1)} reshape(bf16[4,1,16,12,4096]{4,3,2,0,1:T(8,128)(2,1)} %copy.29) | data formatting | bytes 12582912 | tf_op jit(solution)/shard_map/reshape | solution.py:56
  322.0 5.0 %fusion.19 = f32[64,4096]{1,0:T(8,128)} fusion(bf16[64,768]{1,0:T(8,128)(2,1)S(1)} %select_reduce_fusion, bf16[768,4096]{1,0:T(8,128)(2,1)} %reshape.13), kind=kOutput, calls=%fused_computation.29 | convolution fusion | flops 402653184 | bytes 7438336 | tf_op jit(solution)/shard_map/dot_general | solution.py:57
  327.0 0.0 reduce-scatter.2.cloned.1.call-update
  327.0 23.0 %reduce-scatter.2.cloned.1.call-done = f32[64,1024]{1,0:T(8,128)} async-done(((f32[64,4096]{1,0:T(8,128)}), f32[64,1024]{1,0:T(8,128)}) %reduce-scatter.2.cloned.1.call-update) | async-done | bytes 262160 | tf_op jit(solution)/shard_map/reduce_scatter | solution.py:58
  350.0 1.6 convert_element_type.37
  (2 shorter events, 0.0 us)
Async XLA Ops:
  6.5 105.5 %all-gather.2.cloned.1.call-start = ((), (), s32[]{:S(2)}) async-start(), calls=%async_computation.3 | async-start | bytes 7864320 | tf_op jit(solution)/shard_map/all_gather | solution.py:44
  158.0 5.7 %copy-start = (s32[64,8]{0,1:T(8,128)S(1)}, s32[64,8]{0,1:T(8,128)}, u32[]{:S(2)}) copy-start(s32[64,8]{0,1:T(8,128)} %param.15) | copy-start | bytes 6148
  158.0 144.3 %all-to-all-start.1 = ((bf16[1,16,48,4096]{3,1,0,2:T(8,128)(2,1)}), bf16[1,16,48,4096]{3,1,0,2:T(8,128)(2,1)}, u32[]{:S(2)}, u32[]{:S(2)}) async-start(bf16[1,16,48,4096]{3,1,0,2:T(8,128)(2,1)} %copy.28), calls=%async_computation.1 | async-start | bytes 12582912 | tf_op jit(solution)/shard_map/all_to_all | solution.py:53
  163.5 186.6 %reduce-scatter.2.cloned.1.call-start = ((), (), s32[]{:S(2)}) async-start(), calls=%async_computation.4 | async-start | bytes 1310720 | tf_op jit(solution)/shard_map/reduce_scatter | solution.py:58
Sparse Core Ops, SparseCore 0:
  66.5 45.4 all-gather.1
  327.1 22.8 reduce-scatter.1
where the time goes:
time: 359 us; the launch traced here: 358 us
  waiting for transfers between devices  207 us (58%)
  blocking collectives  48.8 us (14%)
  matrix products  44.7 us (12%)
  local copies, waits for them, and re-layouts  34 us (9%)
  between operations  13.5 us (4%)
  starting transfers between devices  5.71 us (2%)
  other arithmetic  5.15 us (1%)
    all_to_all x1, waiting for transfers between devices, on_device(): lax.all_to_all(partial_value[None], 'expert', split_axis=2, concat_axis=0...  138 us
    all_gather x1, waiting for transfers between devices, on_device(): block_cols = lax.all_gather(received, 'hidden', axis=2, tiled=True)  45.7 us
    all_to_all x1, blocking collectives, on_device(): lax.all_to_all(outgoing, 'expert', split_axis=0, concat_axis=2, tiled=True)  40.4 us
    reduce_scatter x1, waiting for transfers between devices, on_device(): lax.psum_scatter(partial_out, 'hidden', scatter_dimension=1, tiled=True)  23 us
    dot_general x1, matrix products, on_device(): jnp.einsum('ehr,ehd->erd', activated, down_proj, preferred_element_type=j...  22.9 us
    dot_general x1, matrix products, on_device(): jnp.einsum('ehd,erd->ehr', gate_proj, block_cols, preferred_element_type=...  14.1 us
    reshape x1, local copies, waits for them, and re-layouts, on_device(): returned = returned.reshape(-1, returned.shape[-1])  9.85 us
    all_to_all x1, local copies, waits for them, and re-layouts, on_device(): lax.all_to_all(partial_value[None], 'expert', split_axis=2, concat_axis=0...  9.84 us
  transfers between devices with their start and end apart: 3, of which 3 were waited for; matrix products, arithmetic and copies ran while one was open for 0% of the time, Pallas kernels for 0%

commit v1 on v0

--- a/solution.py
+++ b/solution.py
@@ -41,7 +41,10 @@
     normed = normalize(tokens, norm_gain, squares)
     outgoing = place_rows(placing, normed, sources)
     received = lax.all_to_all(outgoing, "expert", split_axis=0, concat_axis=2, tiled=True)[0]
-    block_cols = lax.all_gather(received, "hidden", axis=2, tiled=True)
+    size = lax.axis_size("hidden")
+    blocks = jnp.stack([received for _ in range(size)])
+    blocks = lax.all_to_all(blocks, "hidden", split_axis=0, concat_axis=0)
+    block_cols = jnp.concatenate(blocks, axis=2)
     gate_more = jnp.einsum(
         "ehd,erd->ehr", gate_proj, block_cols, preferred_element_type=jnp.float32
     )

time: 359 us -> 389 us (1.084)
  blocking collectives: 48.8 us -> 122 us
  waiting for transfers between devices: 207 us -> 160 us
    all_to_all x0 -> x1, blocking collectives: none -> 73.3 us  [on_device(): blocks = lax.all_to_all(blocks, 'hidden', split_axis=0, concat_axis=0)]
    all_gather x1 -> x0, waiting for transfers between devices: 45.7 us -> none  [on_device(): block_cols = lax.all_gather(received, 'hidden', axis=2, tiled=True)]
  transfers between devices with their start and end apart: 3 -> 2, of which waited for: 3 -> 2; matrix products, arithmetic and copies ran while one was open for 0% -> 0% of each run, Pallas kernels for 0% -> 0%
where the time goes in v1:
time: 389 us; the launch traced here: 388 us
  waiting for transfers between devices  160 us (41%)
  blocking collectives  122 us (31%)
  matrix products  44.8 us (12%)
  local copies, waits for them, and re-layouts  37 us (10%)
  between operations  13.5 us (3%)
  starting transfers between devices  5.71 us (1%)
  other arithmetic  5.15 us (1%)
    all_to_all x1, waiting for transfers between devices, on_device(): lax.all_to_all(partial_value[None], 'expert', split_axis=2, concat_axis=0...  137 us
    all_to_all x1, blocking collectives, on_device(): blocks = lax.all_to_all(blocks, 'hidden', split_axis=0, concat_axis=0)  73.3 us
    all_to_all x1, blocking collectives, on_device(): lax.all_to_all(outgoing, 'expert', split_axis=0, concat_axis=2, tiled=True)  40.4 us
    reduce_scatter x1, waiting for transfers between devices, on_device(): lax.psum_scatter(partial_out, 'hidden', scatter_dimension=1, tiled=True)  23.2 us
    dot_general x1, matrix products, on_device(): jnp.einsum('ehr,ehd->erd', activated, down_proj, preferred_element_type=j...  23 us
    dot_general x1, matrix products, on_device(): jnp.einsum('ehd,erd->ehr', gate_proj, block_cols, preferred_element_type=...  14.1 us
    reshape x1, local copies, waits for them, and re-layouts, on_device(): returned = returned.reshape(-1, returned.shape[-1])  9.85 us
    all_to_all x1, local copies, waits for them, and re-layouts, on_device(): lax.all_to_all(partial_value[None], 'expert', split_axis=2, concat_axis=0...  9.84 us
  transfers between devices with their start and end apart: 2, of which 2 were waited for; matrix products, arithmetic and copies ran while one was open for 0% of the time, Pallas kernels for 0%

profile of v1, /device:TPU:0, one launch (start us, length us, event | category | flops | bytes accessed | tf_op | source)
XLA Modules:
  0.0 388.4 jit_solution(17168114448860215463)
XLA Ops:
  6.5 0.7 multiply_add_fusion
  7.2 0.1 copy.24
  7.3 0.5 fusion.1
  7.9 0.7 convert_element_type.32
  8.6 1.0 fusion.10
  9.6 8.4 %psum.7 = f32[64]{0:T(128)S(1)} all-reduce(f32[64]{0:T(128)S(1)} %fusion.10), channel_id=1, replica_groups=mesh['groups'=2,'expert'=4,'hidden'=4] {'hidden'}, use_global_device_ids=true, to_apply=%region_3.4 | all-reduce | flops 64 | bytes 512 | tf_op jit(solution)/shard_map/psum | solution.py:40
  18.0 2.7 convolution_convert_fusion.1
  20.7 2.4 reshape.19
  23.1 0.9 copy.26
  23.9 40.4 %all_to_all.38 = bf16[4,16,12,1024]{3,1,2,0:T(8,128)(2,1)S(1)} all-to-all(bf16[4,16,12,1024]{3,1,2,0:T(8,128)(2,1)S(1)} %copy.26), channel_id=1, replica_groups=mesh['groups'=2,'expert'=4,'hidden'=4] {'expert'}, dimensions={0} | all-to-all | bytes 3145728 | tf_op jit(solution)/shard_map/all_to_all | solution.py:43
  64.4 0.9 copy.27
  65.2 0.9 stack.3
  66.1 73.3 %all_to_all.39 = bf16[4,16,48,1024]{3,2,1,0:T(8,128)(2,1)S(1)} all-to-all(bf16[4,16,48,1024]{3,2,1,0:T(8,128)(2,1)S(1)} %stack.3), channel_id=1, replica_groups=mesh['groups'=2,'expert'=4,'hidden'=4] {'hidden'}, dimensions={0} | all-to-all | bytes 12582912 | tf_op jit(solution)/shard_map/all_to_all | solution.py:46
  139.4 3.4 copy.31
  142.7 14.1 %convolution_bitcast_fusion.1 = f32[16,192,48]{1,2,0:T(8,128)S(1)} fusion(bf16[16,48,4096]{2,1,0:T(8,128)(2,1)} %bitcast.33, bf16[16,192,4096]{2,1,0:T(8,128)(2,1)} %param.10), kind=kOutput, calls=%fused_computation.7 | convolution fusion | flops 1207959552 | bytes 32047104 | tf_op jit(solution)/shard_map/ehd,erd->ehr/dot_general | solution.py:48
  156.9 23.0 %fusion = bf16[1,16,48,4096]{3,2,1,0:T(8,128)(2,1)} fusion(bf16[16,192,4096]{2,1,0:T(8,128)(2,1)} %param.12, bf16[16,48,4096]{2,1,0:T(8,128)(2,1)} %bitcast.34, bf16[16,192,4096]{2,1,0:T(8,128)(2,1)} %param.11, f32[16,192,48]{1,2,0:T(8,128)S(1)} %convolution_bitcast_fusion.1), kind=kOutput, calls=%fused_computation.1 | convolution fusion | flops 2419949568 | bytes 63504384 | tf_op jit(solution)/shard_map/ehr,ehd->erd/dot_general | solution.py:53
  179.8 8.8 %copy.29 = bf16[1,16,48,4096]{3,1,0,2:T(8,128)(2,1)} copy(bf16[1,16,48,4096]{3,2,1,0:T(8,128)(2,1)} %fusion) | data formatting | bytes 12582912 | tf_op jit(solution)/shard_map/broadcast_in_dim | solution.py:57
  188.6 0.0 copy-start
  188.6 5.4 %all-to-all-start.2 = ((bf16[1,16,48,4096]{3,1,0,2:T(8,128)(2,1)}), bf16[1,16,48,4096]{3,1,0,2:T(8,128)(2,1)}, u32[]{:S(2)}, u32[]{:S(2)}) async-start(bf16[1,16,48,4096]{3,1,0,2:T(8,128)(2,1)} %copy.29), calls=%async_computation.2 | async-start | bytes 12582912 | tf_op jit(solution)/shard_map/all_to_all | solution.py:56
  194.1 0.3 reduce-scatter.2.cloned.1.call-start
  194.3 0.0 copy-done
  194.4 0.1 copy.25
  194.4 0.6 select_reduce_fusion
  195.0 137.1 %all-to-all-done.2 = bf16[1,16,48,4096]{3,1,0,2:T(8,128)(2,1)} async-done(((bf16[1,16,48,4096]{3,1,0,2:T(8,128)(2,1)}), bf16[1,16,48,4096]{3,1,0,2:T(8,128)(2,1)}, u32[]{:S(2)}, u32[]{:S(2)}) %all-to-all-start.2) | async-done | bytes 6291488 | tf_op jit(solution)/shard_map/all_to_all | solution.py:56
  332.1 9.8 %copy.30 = bf16[4,1,16,12,4096]{4,3,2,0,1:T(8,128)(2,1)} copy(bf16[4,1,16,12,4096]{4,2,3,0,1:T(8,128)(2,1)} %bitcast.8) | data formatting | bytes 12582912 | tf_op jit(solution)/shard_map/all_to_all | solution.py:56
  342.0 9.9 %reshape.22 = bf16[768,4096]{1,0:T(8,128)(2,1)} reshape(bf16[4,1,16,12,4096]{4,3,2,0,1:T(8,128)(2,1)} %copy.30) | data formatting | bytes 12582912 | tf_op jit(solution)/shard_map/reshape | solution.py:59
  351.8 5.0 %fusion.19 = f32[64,4096]{1,0:T(8,128)} fusion(bf16[64,768]{1,0:T(8,128)(2,1)S(1)} %select_reduce_fusion, bf16[768,4096]{1,0:T(8,128)(2,1)} %reshape.22), kind=kOutput, calls=%fused_computation.29 | convolution fusion | flops 402653184 | bytes 7438336 | tf_op jit(solution)/shard_map/dot_general | solution.py:60
  356.8 0.0 reduce-scatter.2.cloned.1.call-update
  356.8 23.2 %reduce-scatter.2.cloned.1.call-done = f32[64,1024]{1,0:T(8,128)} async-done(((f32[64,4096]{1,0:T(8,128)}), f32[64,1024]{1,0:T(8,128)}) %reduce-scatter.2.cloned.1.call-update) | async-done | bytes 262160 | tf_op jit(solution)/shard_map/reduce_scatter | solution.py:61
  380.0 1.6 convert_element_type.37
  (2 shorter events, 0.0 us)
Async XLA Ops:
  188.6 5.7 %copy-start = (s32[64,8]{0,1:T(8,128)S(1)}, s32[64,8]{0,1:T(8,128)}, u32[]{:S(2)}) copy-start(s32[64,8]{0,1:T(8,128)} %param.15) | copy-start | bytes 6148
  188.6 143.5 %all-to-all-start.2 = ((bf16[1,16,48,4096]{3,1,0,2:T(8,128)(2,1)}), bf16[1,16,48,4096]{3,1,0,2:T(8,128)(2,1)}, u32[]{:S(2)}, u32[]{:S(2)}) async-start(bf16[1,16,48,4096]{3,1,0,2:T(8,128)(2,1)} %copy.29), calls=%async_computation.2 | async-start | bytes 12582912 | tf_op jit(solution)/shard_map/all_to_all | solution.py:56
  194.1 185.9 %reduce-scatter.2.cloned.1.call-start = ((), (), s32[]{:S(2)}) async-start(), calls=%async_computation.4 | async-start | bytes 1310720 | tf_op jit(solution)/shard_map/reduce_scatter | solution.py:61
Sparse Core Ops, SparseCore 0:
  356.9 22.9 reduce-scatter.1
